TPU v7x, 32 devices: a whole 2x2x4 slice. The times are simulated.
32 devices in a mesh: lat: 8 (over y, x, core), lon: 4 (over z).
Axes of the slice: x: 2, y: 2, z: 4, core: 2. Of those that a mesh axis runs over, the one named last changes fastest.
Arguments:
- velocity: bfloat16 [16, 1024, 512], P(None, 'lat', 'lon'), may hold values from -6 to 6
- theta: bfloat16 [16, 1024, 512], P(None, 'lat', 'lon'), may hold values from -6 to 6
- dx_cell: float32 [1024, 512], P('lat', 'lon'), may hold values from 0.5 to 2
- wet_levels: int32 [1024, 512], P('lat', 'lon'), may hold values from 0 to 16
- bottom_index: int32 [1024, 512], P('lat', 'lon'), may hold values from 1 to 4
- basin_id: int32 [1024, 512], P('lat', 'lon'), may hold values from 0 to 9
- layer_dz: float32 [16], replicated, may hold values from 0.5 to 2
Outputs:
- overturning: float32 [2, 10, 16, 1024], P(None, None, 'lon', 'lat')
All inputs are finite; a program needn't handle non-finite values.
Results may differ from a plain program's by a relative error of at most 0.0003.
Values sent between devices are 32-bit elements; how exact they have to be, the bound alone decides.
A program may use at most 64 MiB of HBM per device.

v0:
```python
import jax
import jax.numpy as jnp
from jax import lax
from jax.sharding import PartitionSpec as P

BASINS = 10


def on_device(velocity, theta, dx_cell, wet_levels, bottom_index, basin_id, layer_dz):
    lon_count = lax.axis_size("lon")
    all_levels = velocity.shape[0]
    basins = BASINS
    scale = 1.0 / (velocity.shape[2] * lon_count) ** 0.5
    bottom_part = bottom_index.astype(jnp.float32) * 0.25
    basin_onehot = (
        basin_id[:, None, :] == jnp.arange(basins, dtype=jnp.int32)[None, :, None]
    ).astype(jnp.float32)
    velocity_rows = velocity.astype(jnp.float32)
    theta_rows = theta.astype(jnp.float32)
    levels = jnp.arange(all_levels, dtype=jnp.int32)
    wet_cells = (levels[:, None, None] < wet_levels[None]).astype(jnp.float32)
    bottom_cells = levels[:, None, None] == wet_levels[None] - 1
    thick = (
        layer_dz[:, None, None]
        * jnp.where(bottom_cells, bottom_part[None], jnp.float32(1.0))
        * wet_cells
    )
    volume = velocity_rows * thick * dx_cell[None]
    heat = volume * theta_rows
    stacked = jnp.stack([volume, heat], axis=1)
    local_running = jnp.cumsum(
        jnp.einsum("kfyx,ybx->kfby", stacked, basin_onehot, precision=lax.Precision.HIGHEST), axis=0
    )
    own_levels = lax.psum_scatter(local_running, "lon", scatter_dimension=0, tiled=True)
    result = own_levels * jnp.float32(scale)
    return jnp.transpose(result, (1, 2, 0, 3))


def solution(mesh):
    placed = (
        P(None, "lat", "lon"),
        P(None, "lat", "lon"),
        P("lat", "lon"),
        P("lat", "lon"),
        P("lat", "lon"),
        P("lat", "lon"),
        P(),
    )
    return jax.shard_map(
        on_device,
        mesh=mesh,
        in_specs=placed,
        out_specs=P(None, None, "lon", "lat"),
        check_vma=False,
    )
```

profile of v0, /device:TPU:0, one launch (start us, length us, event | category | flops | bytes accessed | tf_op | source)
XLA Modules:
  0.0 51.1 jit_solution(5545823323883682771)
XLA Ops:
  6.5 0.0 copy-start
  6.5 0.0 reduce-scatter.2.cloned.1.call-start
  6.5 0.9 %convert_multiply_fusion = f32[128,128]{1,0:T(8,128)S(1)} fusion(s32[128,128]{1,0:T(8,128)} %param.11), kind=kLoop, calls=%fused_computation.14 | loop fusion | flops 32768 | bytes 131072 | tf_op jit(solution)/shard_map/mul | solution.py:14
  7.4 0.8 %broadcast_add_fusion = s32[128,128]{1,0:T(8,128)S(1)} fusion(s32[128,128]{1,0:T(8,128)} %param.10), kind=kLoop, calls=%fused_computation.15 | loop fusion | flops 16384 | bytes 131072 | tf_op jit(solution)/shard_map/sub | solution.py:22
  8.3 2.1 %fusion.9 = (f32[16,1,128,128]{3,0,1,2:T(8,128)S(1)}, f32[16,1,128,128]{3,0,1,2:T(8,128)S(1)}) fusion(f32[128,128]{1,0:T(8,128)} %param.9, f32[128,128]{1,0:T(8,128)S(1)} %convert_multiply_fusion, s32[128,128]{1,0:T(8,128)S(1)} %broadcast_add_fusion, f32[16]{0:T(128)} %param.13, s32[128,128]{1,0:T(8,128)} %param.10, bf16[16,128,128]{2,1,0:T(8,128)(2,1)} %param.7, ...), kind=kLoop, calls=%fused_computation.11 | loop fusion | flops 2621440 | bytes 3407936 | tf_op jit(solution)/shard_map/stack | solution.py:30
  10.4 0.0 copy-done
  10.4 7.4 %fusion.4 = f32[16,2,10,128]{0,2,1,3:T(8,128)S(1)} fusion(f32[16,1,128,128]{3,0,1,2:T(8,128)S(1)} %get-tuple-element.6, f32[16,1,128,128]{3,0,1,2:T(8,128)S(1)} %get-tuple-element.5, s32[128,128]{1,0:T(8,128)S(1)} %copy-done), kind=kOutput, calls=%fused_computation.4 | convolution fusion | flops 63602688 | bytes 2326528 | tf_op jit(solution)/shard_map/kfyx,ybx->kfby/dot_general | solution.py:32
  17.8 1.3 %copy.11 = f32[16,2,10,128]{3,2,1,0:T(8,128)S(1)} copy(f32[16,2,10,128]{0,2,1,3:T(8,128)S(1)} %fusion.4) | data formatting | bytes 327680 | tf_op jit(solution)/shard_map/kfyx,ybx->kfby/transpose | solution.py:32
  19.2 0.7 %fusion.12 = f32[16,2,10,128]{3,2,1,0:T(8,128)} fusion(f32[16,2,10,128]{3,2,1,0:T(8,128)S(1)} %copy.11), kind=kOutput, calls=%fused_computation.17 | output fusion | flops 614400 | bytes 327680 | tf_op jit(solution)/shard_map/jit(cumsum)/reduce_window_sum | solution.py:31
  19.9 0.0 reduce-scatter.2.cloned.1.call-update
  19.9 22.9 %reduce-scatter.2.cloned.1.call-done = f32[4,2,10,128]{3,2,1,0:T(8,128)} async-done(((f32[16,2,10,128]{3,2,1,0:T(8,128)}), f32[4,2,10,128]{3,2,1,0:T(8,128)}) %reduce-scatter.2.cloned.1.call-update) | async-done | bytes 40976 | tf_op jit(solution)/shard_map/reduce_scatter | solution.py:34
  42.8 0.8 %multiply_bitcast_fusion.1 = f32[2,10,4,128]{3,1,0,2:T(8,128)S(1)} fusion(f32[4,2,10,128]{3,2,1,0:T(8,128)} %reduce-scatter.2.cloned.1.call-done), kind=kLoop, calls=%fused_computation.13 | loop fusion | flops 10240 | bytes 81920 | tf_op jit(solution)/shard_map/transpose | solution.py:36
  43.6 0.6 %copy.12 = f32[2,10,4,128]{3,2,1,0:T(4,128)} copy(f32[2,10,4,128]{3,1,0,2:T(8,128)S(1)} %multiply_bitcast_fusion.1) | data formatting | bytes 81920 | tf_op jit(solution)/shard_map/transpose | solution.py:36
Async XLA Ops:
  6.5 3.9 %copy-start = (s32[128,128]{1,0:T(8,128)S(1)}, s32[128,128]{1,0:T(8,128)}, u32[]{:S(2)}) copy-start(s32[128,128]{1,0:T(8,128)} %param.12) | copy-start | bytes 196612
  6.5 36.3 %reduce-scatter.2.cloned.1.call-start = ((), (), s32[]{:S(2)}) async-start(), calls=%async_computation.1 | async-start | bytes 327680 | tf_op jit(solution)/shard_map/reduce_scatter | solution.py:34
Sparse Core Ops, SparseCore 0:
  20.0 22.7 reduce-scatter.1
where the time goes:
time: 51.4 us; the launch traced here: 51.1 us
  waiting for transfers between devices  22.9 us (45%)
  between operations  13.4 us (26%)
  matrix products  7.42 us (14%)
  other arithmetic  5.41 us (11%)
  local copies, waits for them, and re-layouts  2 us (4%)
    reduce_scatter x1, waiting for transfers between devices, on_device(): lax.psum_scatter(local_running, 'lon', scatter_dimension=0, tiled=True)  22.9 us
    dot_general x1, matrix products, on_device(): jnp.einsum('kfyx,ybx->kfby', stacked, basin_onehot, precision=lax.Precisi...  7.42 us
    another operation x1, other arithmetic, on_device(): stacked = jnp.stack([volume, heat], axis=1)  2.12 us
    transpose x1, local copies, waits for them, and re-layouts, on_device(): jnp.einsum('kfyx,ybx->kfby', stacked, basin_onehot, precision=lax.Precisi...  1.35 us
  transfers between devices with their start and end apart: 1, of which 1 were waited for; matrix products, arithmetic and copies ran while one was open for 0% of the time, Pallas kernels for 0%

commit v1 on v0

v1 whole, which is shorter than its diff:
```python
import functools

import jax
import jax.numpy as jnp
from jax import lax
from jax.experimental import pallas as pl
from jax.experimental.pallas import tpu as pltpu
from jax.sharding import PartitionSpec as P

BASINS = 10
SUB = 8


def diagonal(parts, row, lane_row):
    half = len(parts) // 2
    while half >= 1:
        low = (lane_row & half) == 0
        stay = ((row & half) == 0) == low
        merged = []
        for j in range(half):
            kept = jnp.where(low, parts[j], parts[j + half])
            moved = jnp.where(low, parts[j + half], parts[j])
            merged.append(jnp.where(stay, kept, rolled(moved, half, row)))
        parts = merged
        half //= 2
    return parts[0]


def rolled(value, half, row):
    if half == SUB // 2:
        return pltpu.roll(value, half, 0)
    up = pltpu.roll(value, half, 0)
    down = pltpu.roll(value, SUB - half, 0)
    return jnp.where((row & half) == 0, down, up)


def kernel(n, per, dz_ref, v_hbm, t_hbm, dx_hbm, wet_hbm, bot_hbm, bas_hbm, out_ref,
           v_ref, t_ref, dx_ref, wet_ref, bot_ref, bas_ref, onehot, send, recv,
           plane_sem, level_sem, send_sem, recv_sem):
    me = lax.axis_index("lon")
    ny, nx = dx_ref.shape
    groups = ny // SUB
    blocks = nx // SUB
    rows = 2 * per

    planes = [
        pltpu.make_async_copy(src, dst, plane_sem.at[i])
        for i, (src, dst) in enumerate(
            ((bas_hbm, bas_ref), (dx_hbm, dx_ref), (wet_hbm, wet_ref), (bot_hbm, bot_ref))
        )
    ]

    def level_copy(d, i):
        src, dst = ((v_hbm, v_ref), (t_hbm, t_ref))[i]
        part = pl.ds(d * per, per)
        return pltpu.make_async_copy(src.at[part], dst.at[part], level_sem.at[d, i])

    for copy in planes:
        copy.start()
    for d in range(n):
        level_copy(d, 0).start()
        level_copy(d, 1).start()

    barrier = pltpu.get_barrier_semaphore()
    for off in range(1, n):
        pl.semaphore_signal(
            barrier, inc=1, device_id={"lon": lax.rem(me + off, n)}, device_id_type=pl.DeviceIdType.MESH
        )

    row = lax.broadcasted_iota(jnp.int32, (SUB, nx), 0)
    lane = lax.broadcasted_iota(jnp.int32, (SUB, nx), 1)
    lane_row = lane % SUB
    lane_block = lane // SUB
    level_row = row % per

    planes[0].wait()
    for g in range(groups):
        basin = bas_ref[g * SUB:(g + 1) * SUB, :]
        hot = jnp.concatenate(
            [(basin == (p - g) % blocks).astype(jnp.float32) for p in range(blocks)], axis=0
        )
        onehot[g] = hot.astype(jnp.bfloat16)
    for copy in planes[1:]:
        copy.wait()
    bot_scale = 0.25

    def remote(d, slot):
        return pltpu.make_async_remote_copy(
            src_ref=send.at[d],
            dst_ref=recv.at[slot],
            send_sem=send_sem.at[d],
            recv_sem=recv_sem.at[slot],
            device_id={"lon": d},
            device_id_type=pl.DeviceIdType.MESH,
        )

    def one_group(d, carry):
        level_copy(d, 0).wait()
        level_copy(d, 1).wait()
        first = d * per
        merged = [jnp.zeros((SUB, nx), jnp.float32)] * BASINS
        for pair in range(groups // 2):
            both = slice(pair * 2 * SUB, (pair + 1) * 2 * SUB)
            v_both = v_ref[pl.ds(first, per), both, :].astype(jnp.float32)
            t_both = t_ref[pl.ds(first, per), both, :].astype(jnp.float32)
            for side in range(2):
                g = pair * 2 + side
                span = slice(g * SUB, (g + 1) * SUB)
                part = slice(side * SUB, (side + 1) * SUB)
                dx = dx_ref[span, :]
                last = wet_ref[span, :] - 1
                dx_last = dx * (bot_ref[span, :].astype(jnp.float32) * bot_scale)
                volumes, heats = [], []
                for k in range(per):
                    width = jnp.where(
                        first + k < last, dx, jnp.where(first + k == last, dx_last, jnp.float32(0.0))
                    )
                    volume = v_both[k, part, :] * width
                    volumes.append(volume)
                    heats.append(volume * t_both[k, part, :])
                values = jnp.concatenate(volumes + heats, axis=0)
                high = values.astype(jnp.bfloat16)
                low = (values - high.astype(jnp.float32)).astype(jnp.bfloat16)
                hot = onehot[g]
                sums = lax.dot_general(
                    jnp.concatenate([high, low], axis=1),
                    jnp.concatenate([hot, hot], axis=1),
                    (((1,), (1,)), ((), ())),
                    preferred_element_type=jnp.float32,
                )
                picked = diagonal([sums[j * SUB:(j + 1) * SUB, :] for j in range(rows)], row, lane_row)
                merged = [
                    jnp.where(lane_block == (g + b) % blocks, picked, merged[b]) for b in range(BASINS)
                ]
        dz = dz_ref[first]
        for k in range(1, per):
            dz = jnp.where(level_row == k, dz_ref[first + k], dz)
        following = []
        for b in range(BASINS):
            total = merged[b] if b == 0 else pltpu.roll(merged[b], nx - b * SUB, 1)
            total = total * dz
            step = 1
            while step < per:
                total = total + jnp.where(level_row >= step, pltpu.roll(total, step, 0), jnp.float32(0.0))
                step *= 2
            total = total + carry[b]
            send[d, b] = total
            following.append(
                jnp.where(
                    row < per,
                    jnp.broadcast_to(total[per - 1:per, :], total.shape),
                    jnp.broadcast_to(total[2 * per - 1:2 * per, :], total.shape),
                )
            )
        if isinstance(d, int):
            if d == 0:
                pl.semaphore_wait(barrier, n - 1)
        else:
            @pl.when(d == 0)
            def _():
                pl.semaphore_wait(barrier, n - 1)

        @pl.when(d != me)
        def _():
            remote(d, me).start()

        return tuple(following)

    zero = tuple(jnp.zeros((SUB, nx), jnp.float32) for _ in range(BASINS))
    lax.fori_loop(0, n, one_group, zero)

    for off in range(1, n):
        remote(lax.rem(me + off, n), me).wait_send()
    total = send[me]
    for off in range(1, n):
        source = lax.rem(me + off, n)
        remote(source, source).wait_recv()
        total = total + recv[source]
    out_ref[...] = total * jnp.float32(1.0 / (nx * n) ** 0.5)


def solution(mesh):
    n = mesh.shape["lon"]

    def on_device(velocity, theta, dx_cell, wet_levels, bottom_index, basin_id, layer_dz):
        levels, ny, nx = velocity.shape
        per = levels // n
        assert 2 * per == SUB and ny == nx and BASINS * SUB <= nx
        anywhere = pl.BlockSpec(memory_space=pl.ANY)
        piece = (BASINS, 2 * per, nx)
        result = pl.pallas_call(
            functools.partial(kernel, n, per),
            out_shape=jax.ShapeDtypeStruct(piece, jnp.float32),
            in_specs=[pl.BlockSpec(memory_space=pltpu.SMEM)] + [anywhere] * 6,
            out_specs=pl.BlockSpec(memory_space=pltpu.VMEM),
            scratch_shapes=[
                pltpu.VMEM((levels, ny, nx), jnp.bfloat16),
                pltpu.VMEM((levels, ny, nx), jnp.bfloat16),
                pltpu.VMEM((ny, nx), jnp.float32),
                pltpu.VMEM((ny, nx), jnp.int32),
                pltpu.VMEM((ny, nx), jnp.int32),
                pltpu.VMEM((ny, nx), jnp.int32),
                pltpu.VMEM((ny // SUB, nx, nx), jnp.bfloat16),
                pltpu.VMEM((n, *piece), jnp.float32),
                pltpu.VMEM((n, *piece), jnp.float32),
                pltpu.SemaphoreType.DMA((4,)),
                pltpu.SemaphoreType.DMA((n, 2)),
                pltpu.SemaphoreType.DMA((n,)),
                pltpu.SemaphoreType.DMA((n,)),
            ],
            compiler_params=pltpu.CompilerParams(collective_id=0, has_side_effects=True),
        )(layer_dz, velocity, theta, dx_cell, wet_levels, bottom_index, basin_id)
        return jnp.transpose(result.reshape(BASINS, 2, per, ny), (1, 0, 2, 3))

    placed = (
        P(None, "lat", "lon"),
        P(None, "lat", "lon"),
        P("lat", "lon"),
        P("lat", "lon"),
        P("lat", "lon"),
        P("lat", "lon"),
        P(),
    )
    return jax.shard_map(
        on_device,
        mesh=mesh,
        in_specs=placed,
        out_specs=P(None, None, "lon", "lat"),
        check_vma=False,
    )
```

time: 51.4 us -> 12.5 us (0.24)
  waiting for transfers between devices: 22.9 us -> 0 us
  between operations: 13.4 us -> 0.01 us
  Pallas kernels: 0 us -> 10.9 us
  matrix products: 7.42 us -> 0 us
  other arithmetic: 5.41 us -> 0 us
  local copies, waits for them, and re-layouts: 2 us -> 1.4 us
    reduce_scatter x1 -> x0, waiting for transfers between devices: 22.9 us -> none  [on_device(): lax.psum_scatter(local_running, 'lon', scatter_dimension=0, tiled=True)]
    pallas_call x0 -> x1, Pallas kernels: none -> 10.9 us  [on_device(): pl.pallas_call(functools.partial(kernel, n, per), out_shape=jax.ShapeDtyp...]
    dot_general x1 -> x0, matrix products: 7.42 us -> none  [on_device(): jnp.einsum('kfyx,ybx->kfby', stacked, basin_onehot, precision=lax.Precisi...]
    another operation x2 -> x0, other arithmetic: 2.84 us -> none  [the longest x1 2.12 us: on_device(): stacked = jnp.stack([volume, heat], axis=1)]
    transpose x2 -> x0, local copies, waits for them, and re-layouts: 1.99 us -> none  [the longest x1 1.35 us: on_device(): jnp.einsum('kfyx,ybx->kfby', stacked, basin_onehot, precision=lax.Precisi...]
    reshape x0 -> x1, local copies, waits for them, and re-layouts: none -> 1.4 us  [on_device(): return jnp.transpose(result.reshape(BASINS, 2, per, ny), (1, 0, 2, 3))]
    mul x1 -> x0, other arithmetic: 0.88 us -> none  [on_device(): bottom_part = bottom_index.astype(jnp.float32) * 0.25]
    transpose x1 -> x0, other arithmetic: 0.85 us -> none  [on_device(): return jnp.transpose(result, (1, 2, 0, 3))]
  transfers between devices with their start and end apart: 1 -> 0, of which waited for: 1 -> 0; matrix products, arithmetic and copies ran while one was open for 0% -> 0% of each run, Pallas kernels for 0% -> 0%
where the time goes in v1:
time: 12.5 us; the launch traced here: 12.3 us
  Pallas kernels  10.9 us (87%)
  local copies, waits for them, and re-layouts  1.4 us (11%)
    pallas_call x1, Pallas kernels, on_device(): pl.pallas_call(functools.partial(kernel, n, per), out_shape=jax.ShapeDtyp...  10.9 us
    reshape x1, local copies, waits for them, and re-layouts, on_device(): return jnp.transpose(result.reshape(BASINS, 2, per, ny), (1, 0, 2, 3))  1.4 us

profile of v1, /device:TPU:0, one launch (start us, length us, event | category | flops | bytes accessed | tf_op | source)
XLA Modules:
  0.0 12.3 jit_solution(5958935764373884499)
XLA Ops:
  0.0 10.9 %shard_map.73 = f32[10,8,128]{2,1,0:T(8,128)} custom-call(f32[16]{0:T(128)} %dz_ref.1, bf16[16,128,128]{2,1,0:T(8,128)(2,1)} %v_hbm.1, bf16[16,128,128]{2,1,0:T(8,128)(2,1)} %t_hbm.1, f32[128,128]{1,0:T(8,128)} %dx_hbm.1, s32[128,128]{1,0:T(8,128)} %wet_hbm.1, s32[128,128]{1,0:T(8,128)} %bot_hbm.1, s32[128,128]{1,0:T(8,128)} %bas_hbm.1), custom_call_target="tpu_custom_call" | custom-call | tf_op jit(solution)/shard_map/pallas_call | solution.py:191
  10.9 1.4 %copy.10 = f32[10,2,4,128]{3,2,0,1:T(4,128)} copy(f32[10,2,4,128]{3,2,1,0:T(4,128)} %bitcast.4) | data formatting | bytes 81920 | tf_op jit(solution)/shard_map/reshape | solution.py:213

commit v2 on v1

--- a/solution.py
+++ b/solution.py
@@ -190,7 +190,7 @@
         piece = (BASINS, 2 * per, nx)
         result = pl.pallas_call(
             functools.partial(kernel, n, per),
-            out_shape=jax.ShapeDtypeStruct(piece, jnp.float32),
+            out_shape=pltpu.VMEM(piece, jnp.float32),
             in_specs=[pl.BlockSpec(memory_space=pltpu.SMEM)] + [anywhere] * 6,
             out_specs=pl.BlockSpec(memory_space=pltpu.VMEM),
             scratch_shapes=[

time: 12.5 us -> 11 us (0.88)
  local copies, waits for them, and re-layouts: 1.4 us -> 0.63 us
  Pallas kernels: 10.9 us -> 10.3 us
    reshape x1, local copies, waits for them, and re-layouts: 1.4 us -> 0.63 us  [on_device(): return jnp.transpose(result.reshape(BASINS, 2, per, ny), (1, 0, 2, 3))]
    pallas_call x1, Pallas kernels: 10.9 us -> 10.3 us  [on_device(): pl.pallas_call(functools.partial(kernel, n, per), out_shape=pltpu.VMEM(pi...]
where the time goes in v2:
time: 11 us; the launch traced here: 10.9 us
  Pallas kernels  10.3 us (94%)
  local copies, waits for them, and re-layouts  0.63 us (6%)
    pallas_call x1, Pallas kernels, on_device(): pl.pallas_call(functools.partial(kernel, n, per), out_shape=pltpu.VMEM(pi...  10.3 us
    reshape x1, local copies, waits for them, and re-layouts, on_device(): return jnp.transpose(result.reshape(BASINS, 2, per, ny), (1, 0, 2, 3))  0.63 us

profile of v2, /device:TPU:0, one launch (start us, length us, event | category | flops | bytes accessed | tf_op | source)
XLA Modules:
  0.0 10.9 jit_solution(18446544177760682812)
XLA Ops:
  0.0 10.3 %shard_map.73 = f32[10,8,128]{2,1,0:T(8,128)S(1)} custom-call(f32[16]{0:T(128)} %dz_ref.1, bf16[16,128,128]{2,1,0:T(8,128)(2,1)} %v_hbm.1, bf16[16,128,128]{2,1,0:T(8,128)(2,1)} %t_hbm.1, f32[128,128]{1,0:T(8,128)} %dx_hbm.1, s32[128,128]{1,0:T(8,128)} %wet_hbm.1, s32[128,128]{1,0:T(8,128)} %bot_hbm.1, s32[128,128]{1,0:T(8,128)} %bas_hbm.1), custom_call_target="tpu_custom_call" | custom-call | tf_op jit(solution)/shard_map/pallas_call | solution.py:191
  10.3 0.6 %copy.10 = f32[10,2,4,128]{3,2,0,1:T(4,128)} copy(f32[10,2,4,128]{3,2,1,0:T(4,128)S(1)} %bitcast.4) | data formatting | bytes 81920 | tf_op jit(solution)/shard_map/reshape | solution.py:213

commit v3 on v2

--- a/solution.py
+++ b/solution.py
@@ -11,31 +11,17 @@
 SUB = 8
 
 
-def diagonal(parts, row, lane_row):
-    half = len(parts) // 2
-    while half >= 1:
-        low = (lane_row & half) == 0
-        stay = ((row & half) == 0) == low
-        merged = []
-        for j in range(half):
-            kept = jnp.where(low, parts[j], parts[j + half])
-            moved = jnp.where(low, parts[j + half], parts[j])
-            merged.append(jnp.where(stay, kept, rolled(moved, half, row)))
-        parts = merged
-        half //= 2
+def choose(parts, spot):
+    bit = 1
+    while len(parts) > 1:
+        odd = (spot & bit) != 0
+        parts = [jnp.where(odd, parts[j + 1], parts[j]) for j in range(0, len(parts), 2)]
+        bit *= 2
     return parts[0]
 
 
-def rolled(value, half, row):
-    if half == SUB // 2:
-        return pltpu.roll(value, half, 0)
-    up = pltpu.roll(value, half, 0)
-    down = pltpu.roll(value, SUB - half, 0)
-    return jnp.where((row & half) == 0, down, up)
-
-
-def kernel(n, per, dz_ref, v_hbm, t_hbm, dx_hbm, wet_hbm, bot_hbm, bas_hbm, out_ref,
-           v_ref, t_ref, dx_ref, wet_ref, bot_ref, bas_ref, onehot, send, recv,
+def kernel(n, per, dz_hbm, v_hbm, t_hbm, dx_hbm, wet_hbm, bot_hbm, bas_hbm, out_ref,
+           dz_ref, v_ref, t_ref, dx_ref, wet_ref, bot_ref, bas_ref, onehot, send, recv,
            plane_sem, level_sem, send_sem, recv_sem):
     me = lax.axis_index("lon")
     ny, nx = dx_ref.shape
@@ -46,7 +32,7 @@
     planes = [
         pltpu.make_async_copy(src, dst, plane_sem.at[i])
         for i, (src, dst) in enumerate(
-            ((bas_hbm, bas_ref), (dx_hbm, dx_ref), (wet_hbm, wet_ref), (bot_hbm, bot_ref))
+            ((bas_hbm, bas_ref), (dx_hbm, dx_ref), (wet_hbm, wet_ref), (bot_hbm, bot_ref), (dz_hbm, dz_ref))
         )
     ]
 
@@ -54,6 +40,12 @@
         src, dst = ((v_hbm, v_ref), (t_hbm, t_ref))[i]
         part = pl.ds(d * per, per)
         return pltpu.make_async_copy(src.at[part], dst.at[part], level_sem.at[d, i])
+
+    barrier = pltpu.get_barrier_semaphore()
+    for off in range(1, n):
+        pl.semaphore_signal(
+            barrier, inc=1, device_id={"lon": lax.rem(me + off, n)}, device_id_type=pl.DeviceIdType.MESH
+        )
 
     for copy in planes:
         copy.start()
@@ -61,15 +53,9 @@
         level_copy(d, 0).start()
         level_copy(d, 1).start()
 
-    barrier = pltpu.get_barrier_semaphore()
-    for off in range(1, n):
-        pl.semaphore_signal(
-            barrier, inc=1, device_id={"lon": lax.rem(me + off, n)}, device_id_type=pl.DeviceIdType.MESH
-        )
-
     row = lax.broadcasted_iota(jnp.int32, (SUB, nx), 0)
     lane = lax.broadcasted_iota(jnp.int32, (SUB, nx), 1)
-    lane_row = lane % SUB
+    source_part = (row - lane) % SUB
     lane_block = lane // SUB
     level_row = row % per
 
@@ -116,8 +102,9 @@
                         first + k < last, dx, jnp.where(first + k == last, dx_last, jnp.float32(0.0))
                     )
                     volume = v_both[k, part, :] * width
-                    volumes.append(volume)
-                    heats.append(volume * t_both[k, part, :])
+                    heat = volume * t_both[k, part, :]
+                    volumes.append(volume if k == 0 else pltpu.roll(volume, k, 0))
+                    heats.append(pltpu.roll(heat, per + k, 0))
                 values = jnp.concatenate(volumes + heats, axis=0)
                 high = values.astype(jnp.bfloat16)
                 low = (values - high.astype(jnp.float32)).astype(jnp.bfloat16)
@@ -128,16 +115,21 @@
                     (((1,), (1,)), ((), ())),
                     preferred_element_type=jnp.float32,
                 )
-                picked = diagonal([sums[j * SUB:(j + 1) * SUB, :] for j in range(rows)], row, lane_row)
+                picked = choose([sums[j * SUB:(j + 1) * SUB, :] for j in range(rows)], source_part)
                 merged = [
                     jnp.where(lane_block == (g + b) % blocks, picked, merged[b]) for b in range(BASINS)
                 ]
         dz = dz_ref[first]
         for k in range(1, per):
             dz = jnp.where(level_row == k, dz_ref[first + k], dz)
+        dz = dz * jnp.float32(1.0 / (nx * n) ** 0.5)
         following = []
         for b in range(BASINS):
             total = merged[b] if b == 0 else pltpu.roll(merged[b], nx - b * SUB, 1)
+            shift = 1
+            while shift < SUB:
+                total = jnp.where((lane & shift) != 0, pltpu.roll(total, SUB - shift, 0), total)
+                shift *= 2
             total = total * dz
             step = 1
             while step < per:
@@ -169,14 +161,14 @@
     zero = tuple(jnp.zeros((SUB, nx), jnp.float32) for _ in range(BASINS))
     lax.fori_loop(0, n, one_group, zero)
 
-    for off in range(1, n):
-        remote(lax.rem(me + off, n), me).wait_send()
     total = send[me]
     for off in range(1, n):
         source = lax.rem(me + off, n)
         remote(source, source).wait_recv()
         total = total + recv[source]
-    out_ref[...] = total * jnp.float32(1.0 / (nx * n) ** 0.5)
+    out_ref[...] = total
+    for off in range(1, n):
+        remote(lax.rem(me + off, n), me).wait_send()
 
 
 def solution(mesh):
@@ -191,9 +183,10 @@
         result = pl.pallas_call(
             functools.partial(kernel, n, per),
             out_shape=pltpu.VMEM(piece, jnp.float32),
-            in_specs=[pl.BlockSpec(memory_space=pltpu.SMEM)] + [anywhere] * 6,
+            in_specs=[anywhere] * 7,
             out_specs=pl.BlockSpec(memory_space=pltpu.VMEM),
             scratch_shapes=[
+                pltpu.SMEM((levels,), jnp.float32),
                 pltpu.VMEM((levels, ny, nx), jnp.bfloat16),
                 pltpu.VMEM((levels, ny, nx), jnp.bfloat16),
                 pltpu.VMEM((ny, nx), jnp.float32),
@@ -203,7 +196,7 @@
                 pltpu.VMEM((ny // SUB, nx, nx), jnp.bfloat16),
                 pltpu.VMEM((n, *piece), jnp.float32),
                 pltpu.VMEM((n, *piece), jnp.float32),
-                pltpu.SemaphoreType.DMA((4,)),
+                pltpu.SemaphoreType.DMA((5,)),
                 pltpu.SemaphoreType.DMA((n, 2)),
                 pltpu.SemaphoreType.DMA((n,)),
                 pltpu.SemaphoreType.DMA((n,)),

time: 11 us -> 10.4 us (0.945)
  Pallas kernels: 10.3 us -> 9.6 us
    pallas_call x1, Pallas kernels: 10.3 us -> 9.6 us  [on_device(): pl.pallas_call(functools.partial(kernel, n, per), out_shape=pltpu.VMEM(pi...]
where the time goes in v3:
time: 10.4 us; the launch traced here: 10.2 us
  Pallas kernels  9.6 us (92%)
  local copies, waits for them, and re-layouts  0.63 us (6%)
    pallas_call x1, Pallas kernels, on_device(): pl.pallas_call(functools.partial(kernel, n, per), out_shape=pltpu.VMEM(pi...  9.6 us
    reshape x1, local copies, waits for them, and re-layouts, on_device(): return jnp.transpose(result.reshape(BASINS, 2, per, ny), (1, 0, 2, 3))  0.63 us

profile of v3, /device:TPU:0, one launch (start us, length us, event | category | flops | bytes accessed | tf_op | source)
XLA Modules:
  0.0 10.2 jit_solution(14584853986330265224)
XLA Ops:
  0.0 9.6 %shard_map.73 = f32[10,8,128]{2,1,0:T(8,128)S(1)} custom-call(f32[16]{0:T(128)} %dz_hbm.1, bf16[16,128,128]{2,1,0:T(8,128)(2,1)} %v_hbm.1, bf16[16,128,128]{2,1,0:T(8,128)(2,1)} %t_hbm.1, f32[128,128]{1,0:T(8,128)} %dx_hbm.1, s32[128,128]{1,0:T(8,128)} %wet_hbm.1, s32[128,128]{1,0:T(8,128)} %bot_hbm.1, s32[128,128]{1,0:T(8,128)} %bas_hbm.1), custom_call_target="tpu_custom_call" | custom-call | tf_op jit(solution)/shard_map/pallas_call | solution.py:183
  9.6 0.6 %copy.10 = f32[10,2,4,128]{3,2,0,1:T(4,128)} copy(f32[10,2,4,128]{3,2,1,0:T(4,128)S(1)} %bitcast.4) | data formatting | bytes 81920 | tf_op jit(solution)/shard_map/reshape | solution.py:206
